TPU v7x, 32 devices: a whole 2x2x4 slice. The times are simulated.
32 devices in a mesh: seq: 8 (over z, y), head: 4 (over x, core).
Axes of the slice: x: 2, y: 2, z: 4, core: 2. Of those that a mesh axis runs over, the one named last changes fastest.
Arguments:
- seq_inputs: bfloat16 [1, 2048, 4096], P(None, 'seq', 'head'), may hold values from -6 to 6
- gate_inputs: bfloat16 [1, 2048, 4096], P(None, 'seq', 'head'), may hold values from -6 to 6
- projections: bfloat16 [1, 2048, 256], P(None, 'seq'), may hold values from -6 to 6
- step_raw: float32 [1, 2048, 64], P(None, 'seq', 'head'), may hold values from -3 to 3
- step_bias: float32 [64], P('head'), may hold values from -1 to 1
- decay_rate: float32 [64], P('head'), may hold values from 0.00048828125 to 8
- conv_feature: float32 [4, 4096], P(None, 'head'), may hold values from -3 to 3
- conv_proj: float32 [4, 256], replicated, may hold values from -3 to 3
- norm_gain: float32 [4096], P('head'), may hold values from 0.25 to 1.75
Outputs:
- mixed_out: bfloat16 [1, 2048, 4096], P(None, 'seq', 'head')
All inputs are finite; a program needn't handle non-finite values.
Results may differ from a plain program's by a relative error of at most 0.0034.
Values may be sent and summed in bfloat16 or wider, within the bound.
A program may use at most 192 MiB of HBM per device.

v0:
```python
import jax
import jax.numpy as jnp
from jax import lax
from jax.sharding import PartitionSpec as P

HEADS = 64
HEAD_DIM = 64
STRETCH = 256


def from_behind(value, axis, steps):
    count = lax.axis_size(axis)
    leading, last = (max(0, -steps), min(count, count - steps))
    return lax.ppermute(value, axis, [(source, source + steps) for source in range(leading, last)])


def entering_2(array, axis, combine, identity):
    count, mine = (lax.axis_size(axis), lax.axis_index(axis))
    everything = jax.tree.map(lambda part: lax.all_gather(part, axis), array)
    start = jax.tree.map(
        lambda part, zero: jnp.broadcast_to(jnp.asarray(zero, part.dtype), part.shape),
        array,
        identity,
    )

    def hop(k, before):
        reached = k < mine
        new = combine(before, jax.tree.map(lambda part: part[k], everything))
        return jax.tree.map(lambda a, b: jnp.where(reached, a, b), new, before)

    return lax.fori_loop(0, count, hop, start)


def causal_mix(window, weights):
    kernel_len = weights.shape[0]
    length = window.shape[1] - kernel_len + 1
    running = window[:, 0:length].astype(jnp.float32) * weights[0]
    for offset in range(1, kernel_len):
        running = (
            running + window[:, offset : offset + length].astype(jnp.float32) * weights[offset]
        )
    return jax.nn.silu(running).astype(jnp.bfloat16)


def block_local(x_mixed, write_vec, read_vec, step_lead, decay_rate):
    flat_count, span, channels = x_mixed.shape
    head_count = decay_rate.shape[0]
    head_width = channels // head_count
    state_size = write_vec.shape[2]
    group_count = head_count // 2
    scores = jnp.einsum("btn,bsn->bts", read_vec, write_vec, preferred_element_type=jnp.float32)
    causal = jnp.arange(span)[:, None] >= jnp.arange(span)[None, :]
    log_lead = jnp.cumsum(step_lead * (-decay_rate)[None, :, None], axis=2)

    def head_group(operands):
        x_group, step_group, log_group = operands
        decay_gap = jnp.where(
            causal[None, None], log_group[:, :, :, None] - log_group[:, :, None, :], 0.0
        )
        mixing = jnp.where(
            causal[None, None],
            scores[:, None] * jnp.exp(decay_gap) * step_group[:, :, None, :],
            0.0,
        ).astype(jnp.bfloat16)
        x_heads = x_group.reshape(flat_count, span, 2, head_width)
        within = jnp.einsum("bhts,bshp->bthp", mixing, x_heads, preferred_element_type=jnp.float32)
        to_end = jnp.exp(log_group[:, :, -1:] - log_group) * step_group
        to_end = jnp.transpose(to_end, (0, 2, 1))
        weighted = (x_heads.astype(jnp.float32) * to_end[:, :, :, None]).astype(jnp.bfloat16)
        summary = jnp.einsum(
            "bshp,bsn->bhpn", weighted, write_vec, preferred_element_type=jnp.float32
        )
        return (within.reshape(flat_count, span, 2 * head_width), summary)

    x_groups = jnp.transpose(
        x_mixed.reshape(flat_count, span, group_count, 2 * head_width), (2, 0, 1, 3)
    )
    step_groups = jnp.transpose(step_lead.reshape(flat_count, group_count, 2, span), (1, 0, 2, 3))
    log_groups = jnp.transpose(log_lead.reshape(flat_count, group_count, 2, span), (1, 0, 2, 3))
    within, summary = lax.map(head_group, (x_groups, step_groups, log_groups))
    within = jnp.transpose(within, (1, 2, 0, 3)).reshape(flat_count, span, channels)
    summary = jnp.transpose(summary, (1, 0, 2, 3, 4)).reshape(
        flat_count, head_count, head_width, state_size
    )
    return (within, summary, log_lead)


def combine(earlier, later):
    return (earlier[0] * later[0], later[0][:, :, None, None] * earlier[1] + later[1])


def shards(
    seq_inputs,
    gate_inputs,
    projections,
    step_raw,
    step_bias,
    decay_rate,
    conv_feature,
    conv_proj,
    norm_gain,
):
    kernel_len = conv_feature.shape[0]
    batch_rows, local_len, channels = seq_inputs.shape
    head_count = decay_rate.shape[0]
    head_width = channels // head_count
    state_size = projections.shape[2] // 2
    block_count = local_len // STRETCH
    flat_count = batch_rows * block_count
    halo_rows = from_behind(
        (seq_inputs[:, local_len - kernel_len + 1 :], projections[:, local_len - kernel_len + 1 :]),
        "seq",
        1,
    )
    x_mixed = causal_mix(jnp.concatenate([halo_rows[0], seq_inputs], axis=1), conv_feature)
    proj_mixed = causal_mix(jnp.concatenate([halo_rows[1], projections], axis=1), conv_proj)
    write_vec = proj_mixed[:, :, :state_size]
    read_vec = proj_mixed[:, :, state_size:]
    step_size = jax.nn.softplus(step_raw + step_bias)
    step_lead = jnp.transpose(step_size, (0, 2, 1))
    within, summary, log_lead = block_local(x_mixed, write_vec, read_vec, step_lead, decay_rate)
    summary = summary.reshape(batch_rows, block_count, head_count, head_width, state_size)
    block_decay = jnp.exp(log_lead[:, :, -1]).reshape(batch_rows, block_count, head_count)
    decay_acc = jnp.ones((batch_rows, head_count), jnp.float32)
    state_acc = jnp.zeros((batch_rows, head_count, head_width, state_size), jnp.float32)
    decay_list = [decay_acc]
    state_list = [state_acc]
    state_acc = block_decay[:, 0, :, None, None] * state_acc + summary[:, 0]
    decay_acc = decay_acc * block_decay[:, 0]
    prior_decay = jnp.stack(decay_list, axis=1)
    prior_state = jnp.stack(state_list, axis=1)
    incoming = entering_2(
        (decay_acc, state_acc),
        "seq",
        combine,
        (jnp.ones_like(decay_acc), jnp.zeros_like(state_acc)),
    )
    entering_state = incoming[1]
    entering = prior_decay[:, :, :, None, None] * entering_state[:, None] + prior_state
    entering = entering.reshape(flat_count, head_count, head_width, state_size).astype(jnp.bfloat16)
    outside = jnp.einsum("bhpn,btn->bthp", entering, read_vec, preferred_element_type=jnp.float32)
    decay_now = jnp.transpose(jnp.exp(log_lead), (0, 2, 1))
    outside = (outside * decay_now[:, :, :, None]).reshape(flat_count, STRETCH, channels)
    total_out = within + outside
    gated = total_out * jax.nn.silu(gate_inputs.astype(jnp.float32))
    squares = lax.psum(jnp.sum(gated * gated, axis=-1), "head")
    scale = lax.rsqrt(squares / (HEADS * HEAD_DIM) + 1.0)
    return (gated * scale[:, :, None] * norm_gain).astype(jnp.bfloat16)


def solution(mesh):
    return jax.shard_map(
        shards,
        mesh=mesh,
        in_specs=(
            P(None, "seq", "head"),
            P(None, "seq", "head"),
            P(None, "seq", None),
            P(None, "seq", "head"),
            P("head"),
            P("head"),
            P(None, "head"),
            P(),
            P("head"),
        ),
        out_specs=P(None, "seq", "head"),
        check_vma=False,
    )
```

profile of v0, /device:TPU:0, one launch (start us, length us, event | category | flops | bytes accessed | tf_op | source)
XLA Modules:
  0.0 133.4 jit_solution(5358744158412909568)
XLA Ops:
  7.2 4.9 %collective-permute-start.1 = (bf16[1,3,256]{2,1,0:T(4,128)(2,1)S(1)}, bf16[1,3,256]{2,1,0:T(4,128)(2,1)S(1)}, u32[]{:S(2)}, u32[]{:S(2)}) collective-permute-start(bf16[1,3,256]{2,1,0:T(4,128)(2,1)S(1)} %slice.74), channel_id=1, source_target_pairs={{0,4},{4,8},{8,12},{12,16},{16,20},{20,24},{24,28},{1,5},{5,9},{9,... | collective-permute-start | bytes 4616 | tf_op jit(solution)/shard_map/ppermute | solution.py:14
  12.9 3.4 %collective-permute-start = (bf16[1,3,1024]{2,1,0:T(4,128)(2,1)S(1)}, bf16[1,3,1024]{2,1,0:T(4,128)(2,1)S(1)}, u32[]{:S(2)}, u32[]{:S(2)}) collective-permute-start(bf16[1,3,1024]{2,1,0:T(4,128)(2,1)S(1)} %slice.66), channel_id=1, source_target_pairs={{0,4},{4,8},{8,12},{12,16},{16,20},{20,24},{24,28},{1,5},{5,9},{9,... | collective-permute-start | bytes 18440 | tf_op jit(solution)/shard_map/ppermute | solution.py:14
  16.9 0.8 multiply_bitcast_fusion
  18.5 0.9 fusion.34
  20.0 0.8 fusion.35
  20.9 1.4 %multiply_convert_fusion.3 = bf16[1,256,256]{2,1,0:T(8,128)(2,1)S(1)} fusion(bf16[1,256,256]{2,1,0:T(8,128)(2,1)} %param.15, bf16[1,3,256]{2,1,0:T(4,128)(2,1)S(1)} %collective-permute-done.1, f32[256]{0:T(256)S(1)} %bitcast.147, f32[256]{0:T(256)S(1)} %bitcast.148, f32[256]{0:T(256)S(1)} %bitcast.146, f32[256]{0:T(256)S(1)} %bitcast.145), kind=kLoop, calls=%fused_computation.47 | loop fusion | flops 1638400 | bytes 267776 | tf_op jit(solution)/shard_map/convert_element_type | solution.py:42
  22.5 2.8 %multiply_convert_fusion.2 = bf16[1,256,1024]{2,1,0:T(8,128)(2,1)S(1)} fusion(bf16[1,256,1024]{2,1,0:T(8,128)(2,1)} %param.13, bf16[1,3,1024]{2,1,0:T(4,128)(2,1)S(1)} %collective-permute-done, f32[1024]{0:T(1024)S(1)} %bitcast.143, f32[1024]{0:T(1024)S(1)} %bitcast.144, f32[1024]{0:T(1024)S(1)} %bitcast.142, f32[1024]{0:T(1024)S(1)} %bitcast.141), kind=kLoop, calls=%fused_computation.38 | loop fusion | flops 6553600 | bytes 1071104 | tf_op jit(solution)/shard_map/convert_element_type | solution.py:42
  25.5 7.3 %while.28 = (s32[]{:T(128)}, f32[8,1,256,128]{2,3,1,0:T(8,128)S(1)}, f32[8,1,2,64,128]{4,3,2,1,0:T(8,128)S(1)}, bf16[8,1,256,128]{2,3,1,0:T(8,128)(2,1)S(1)}, f3...) while((s32[]{:T(128)}, ...), condition=%wide.region_3.4_spmd.clone.clone, body=%wide.region_2.3_spmd.clone.clone.sunk | while | flops 26117120 | bytes 1534093 | solution.py:80
  32.8 0.9 broadcast_add_fusion
  33.8 18.3 %all-gather = f32[8,16,1]{1,2,0:T(1,128)S(1)} all-gather(f32[1,16,1]{1,2,0:T(1,128)S(1)} %copy.63), channel_id=2, replica_groups=mesh['seq'=8,'head'=4] {'seq'}, dimensions={0}, use_global_device_ids=true | all-gather | bytes 576 | tf_op jit(solution)/shard_map/all_gather | solution.py:19
  52.4 54.5 %all-gather.3.cloned.1.call-done = f32[8,1,16,64,128]{4,3,2,1,0:T(8,128)} async-done(((f32[1,1,16,64,128]{4,3,2,1,0:T(8,128)}), f32[8,1,16,64,128]{4,3,2,1,0:T(8,128)}) %all-gather.3.cloned.1.call-update) | async-done | bytes 4194320 | tf_op jit(solution)/shard_map/all_gather | solution.py:19
  106.9 9.7 %while.29 = (s32[]{:T(128)}, f32[1,16,64,128]{3,2,1,0:T(8,128)S(1)}, s32[]{:T(128)}, f32[8,1,16]{2,1,0:T(1,128)S(1)}, f32[8,1,16,64,128]{4,3,2,1,0:T(8,128)}, /*index=5*/s32[]{:T(128)}, s32[]{:T(128)}) while((s32[]{:T(128)}, f32[1,16,64,128]{3,2,1,0:T(8,128)S(1)}, s32[]{:T(128)}, f32[8,1,16]{2,1,0:T(1,128)S(1)}, ...), condition=%wide.region_5.6_spmd.clone, body=%wide.region_4.5_spmd.clone.sunk | while | flops 524292 | bytes 1573161 | solution.py:31
  106.9 1.2 fusion.51
  108.2 1.2 fusion.51
  109.4 1.2 fusion.51
  110.6 1.2 fusion.51
  111.8 1.2 fusion.51
  113.0 1.2 fusion.51
  114.3 1.2 fusion.51
  115.5 1.2 fusion.51
  117.0 1.3 copy.65
  118.3 1.6 %multiply_reduce_fusion = (f32[256]{0:T(256)S(1)}, f32[1,256,1024]{2,1,0:T(8,128)S(1)}) fusion(bf16[1,256,1024]{2,1,0:T(8,128)(2,1)S(1)} %copy-done, f32[1,256,1024]{2,1,0:T(8,128)S(1)} %copy.67, f32[1,256,1024]{2,1,0:T(8,128)} %copy.65), kind=kLoop, calls=%fused_computation.37 | loop fusion | flops 2359040 | bytes 3671040 | tf_op jit(solution)/shard_map/reduce_sum | solution.py:146
  119.9 5.7 %psum.7 = f32[1,256]{1,0:T(1,128)S(1)} all-reduce(f32[1,256]{1,0:T(1,128)S(1)} %bitcast.152), channel_id=1, replica_groups=mesh['seq'=8,'head'=4] {'head'}, use_global_device_ids=true, to_apply=%region_7.8 | all-reduce | flops 256 | bytes 2048 | tf_op jit(solution)/shard_map/psum | solution.py:146
  125.6 1.0 multiply_convert_fusion.1
  (122 shorter events, 11.3 us)
Async XLA Ops:
  6.5 100.4 %all-gather.3.cloned.1.call-start = ((), (), s32[]{:S(2)}) async-start(), calls=%async_computation | async-start | bytes 4718592 | tf_op jit(solution)/shard_map/all_gather | solution.py:19
  7.2 13.6 %collective-permute-start.1 = (bf16[1,3,256]{2,1,0:T(4,128)(2,1)S(1)}, bf16[1,3,256]{2,1,0:T(4,128)(2,1)S(1)}, u32[]{:S(2)}, u32[]{:S(2)}) collective-permute-start(bf16[1,3,256]{2,1,0:T(4,128)(2,1)S(1)} %slice.74), channel_id=1, source_target_pairs={{0,4},{4,8},{8,12},{12,16},{16,20},{20,24},{24,28},{1,5},{5,9},{9,... | collective-permute-start | bytes 4616 | tf_op jit(solution)/shard_map/ppermute | solution.py:14
  12.9 9.6 %collective-permute-start = (bf16[1,3,1024]{2,1,0:T(4,128)(2,1)S(1)}, bf16[1,3,1024]{2,1,0:T(4,128)(2,1)S(1)}, u32[]{:S(2)}, u32[]{:S(2)}) collective-permute-start(bf16[1,3,1024]{2,1,0:T(4,128)(2,1)S(1)} %slice.66), channel_id=1, source_target_pairs={{0,4},{4,8},{8,12},{12,16},{16,20},{20,24},{24,28},{1,5},{5,9},{9,... | collective-permute-start | bytes 18440 | tf_op jit(solution)/shard_map/ppermute | solution.py:14
  106.9 11.4 %copy-start = (bf16[1,256,1024]{2,1,0:T(8,128)(2,1)S(1)}, bf16[1,256,1024]{2,1,0:T(8,128)(2,1)}, u32[]{:S(2)}) copy-start(bf16[1,256,1024]{2,1,0:T(8,128)(2,1)} %param.14) | copy-start | bytes 1572868
  116.6 9.0 %copy-start.1 = (f32[1024]{0:T(1024)S(1)}, f32[1024]{0:T(1024)}, u32[]{:S(2)}) copy-start(f32[1024]{0:T(1024)} %param.21) | copy-start | bytes 12292
Sparse Core Ops, SparseCore 0:
  33.8 73.0 all-gather.2
where the time goes:
time: 134 us; the launch traced here: 133 us
  waiting for transfers between devices  54.5 us (41%)
  blocking collectives  23.9 us (18%)
  other arithmetic  20.6 us (15%)
  between operations  13.5 us (10%)
  starting transfers between devices  8.31 us (6%)
  local copies, waits for them, and re-layouts  7.38 us (6%)
  matrix products  4.33 us (3%)
    all_gather x1, waiting for transfers between devices, entering_2(): everything = jax.tree.map(lambda part: lax.all_gather(part, axis), array)  54.5 us
    all_gather x1, blocking collectives, entering_2(): everything = jax.tree.map(lambda part: lax.all_gather(part, axis), array)  18.3 us
    select_n x8, other arithmetic, hop(): return jax.tree.map(lambda a, b: jnp.where(reached, a, b), new, before)  9.43 us
    ppermute x2, starting transfers between devices, from_behind(): lax.ppermute(value, axis, [(source, source + steps) for source in range(l...  8.3 us
    psum x1, blocking collectives, shards(): squares = lax.psum(jnp.sum(gated * gated, axis=-1), 'head')  5.66 us
    convert_element_type x2, other arithmetic, causal_mix(): return jax.nn.silu(running).astype(jnp.bfloat16)  4.18 us
    dot_general x8, matrix products, head_group(): jnp.einsum('bhts,bshp->bthp', mixing, x_heads, preferred_element_type=jnp...  2.7 us
  transfers between devices with their start and end apart: 3, of which 1 were waited for; matrix products, arithmetic and copies ran while one was open for 5% of the time, Pallas kernels for 0%

commit v1 on v0

v1 whole, which is shorter than its diff:
```python
import functools
import math

import jax
import jax.numpy as jnp
from jax import lax
from jax.experimental import pallas as pl
from jax.experimental.pallas import tpu as pltpu
from jax.sharding import PartitionSpec as P

HEADS = 64
HEAD_DIM = 64
STRETCH = 256
LANES = 128
LOG2E = math.log2(math.e)
MESH = pl.DeviceIdType.MESH


def silu(value):
    half = 0.5 * value
    return half + half * jnp.tanh(half)


def pieces(value, count):
    parts = []
    for _ in range(count):
        part = value.astype(jnp.bfloat16)
        parts.append(part)
        value = value - part.astype(jnp.float32)
    return parts


def dot(a, b):
    return jnp.dot(a, b, preferred_element_type=jnp.float32)


def dot_parts(parts, b):
    total = dot(parts[-1], b)
    for part in parts[-2::-1]:
        total = total + dot(part, b)
    return total


def iota(shape, dim):
    return lax.broadcasted_iota(jnp.int32, shape, dim)


def conv(wide, slot, halo, rows, weights):
    span = rows.shape[0]
    taps = weights.shape[0]
    wide[slot, 0:8] = halo.astype(jnp.float32)
    wide[slot, 8 : 8 + span] = rows.astype(jnp.float32)
    first = 8 - taps + 1
    total = wide[slot, first : first + span] * weights[0:1]
    for k in range(1, taps):
        total = total + wide[slot, first + k : first + k + span] * weights[k : k + 1]
    return silu(total)


def kernel(
    n,
    m,
    total_channels,
    x_hbm,
    gate_hbm,
    proj_hbm,
    raw_hbm,
    bias_ref,
    rate_ref,
    cf_ref,
    cp_ref,
    gain_ref,
    out_ref,
    x_v,
    gate_v,
    proj_v,
    raw_v,
    halo_x,
    halo_p,
    wide_x,
    wide_p,
    pad,
    m_t,
    xm,
    within,
    s_send,
    s_recv,
    s_own,
    d_own,
    d_recv,
    p_in,
    p_out,
    e_own,
    e_send,
    e_recv,
    sq_send,
    sq_recv,
    x_sem,
    gate_sem,
    misc_sem,
    halo_s,
    halo_r,
    d_s,
    d_r,
    s_s,
    s_r,
    p_s,
    p_r,
    e_s,
    e_r,
    sq_s,
    sq_r,
):
    span = proj_v.shape[1]
    chunks = x_v.shape[0]
    half = chunks // 2
    heads = rate_ref.shape[1]
    per = heads // chunks
    width = LANES // per
    i = lax.axis_index("seq")
    hd = lax.axis_index("head")
    y = lax.rem(i, 2)
    partner = i + 1 - 2 * y
    has_prev, has_next = i > 0, i < n - 1
    has_before, has_after = i >= 2, i < n - 2

    barrier = pltpu.get_barrier_semaphore()
    relations = [(has_prev, i - 1), (has_next, i + 1), (has_before, i - 2), (has_after, i + 2)]
    for here, who in relations:

        @pl.when(here)
        def _():
            pl.semaphore_signal(barrier, inc=1, device_id=(who, hd), device_id_type=MESH)

    for k in range(1, m):
        pl.semaphore_signal(
            barrier, inc=1, device_id=(i, lax.rem(hd + k, m)), device_id_type=MESH
        )

    raw_copy = pltpu.make_async_copy(raw_hbm, raw_v, misc_sem.at[0])
    raw_copy.start()
    proj_copies = [
        pltpu.make_async_copy(
            proj_hbm.at[:, k * LANES : (k + 1) * LANES], proj_v.at[k], misc_sem.at[1 + k]
        )
        for k in range(2)
    ]
    for copy in proj_copies:
        copy.start()
    x_copies = []
    gate_copies = []
    for c in range(chunks):
        cols = slice(c * LANES, (c + 1) * LANES)
        x_copies.append(pltpu.make_async_copy(x_hbm.at[:, cols], x_v.at[c], x_sem.at[c]))
        gate_copies.append(
            pltpu.make_async_copy(gate_hbm.at[:, cols], gate_v.at[c], gate_sem.at[c])
        )
    for copy in x_copies + gate_copies:
        copy.start()

    pl.semaphore_wait(barrier, sum(here.astype(jnp.int32) for here, _ in relations) + m - 1)

    halo_rows = halo_x.shape[0]
    halos = [
        pltpu.make_async_remote_copy(
            src_ref=src.at[span - halo_rows : span],
            dst_ref=dst,
            send_sem=halo_s.at[k],
            recv_sem=halo_r.at[k],
            device_id=(lax.rem(i + 1, n), hd),
            device_id_type=MESH,
        )
        for k, (src, dst) in enumerate([(x_hbm, halo_x), (proj_hbm, halo_p)])
    ]

    @pl.when(has_next)
    def _():
        for copy in halos:
            copy.start()

    raw_copy.wait()
    shifted = raw_v[...] + bias_ref[...]
    step = jnp.maximum(shifted, 0.0) + jnp.log1p(jnp.exp(-jnp.abs(shifted)))
    tri = (iota((span, span), 0) >= iota((span, span), 1)).astype(jnp.bfloat16)
    lead = (step * (-LOG2E)) * rate_ref[...]
    run = None
    for part in reversed(pieces(lead, 3)):
        term = dot(tri, part)
        run = term if run is None else run + term
    source = run - LOG2E * jnp.log(step)
    last = run[span - 1 : span]
    to_end = pieces(jnp.exp2(last - source), 2)
    decay_now = pieces(jnp.exp2(run), 2)
    pad[...] = jnp.zeros_like(pad)
    pad[:, 0:heads] = source
    m_t[...] = jnp.transpose(pad[...])

    def spread(parts, c):
        pick = iota((heads, LANES), 0) == c * per + iota((heads, LANES), 1) // width
        return dot_parts(parts, pick.astype(jnp.bfloat16))

    owner = iota((chunks, heads), 1) // per == iota((chunks, heads), 0)
    ends = jnp.where(owner, jnp.broadcast_to(jnp.exp2(last), (chunks, heads)), 0.0)
    lane_of = iota((heads, LANES), 0) % per == iota((heads, LANES), 1) // width
    d_own[...] = dot_parts(pieces(ends, 3), lane_of.astype(jnp.bfloat16))

    def to_partner(src, dst, send_sem, recv_sem):
        return pltpu.make_async_remote_copy(
            src_ref=src,
            dst_ref=dst,
            send_sem=send_sem,
            recv_sem=recv_sem,
            device_id=(partner, hd),
            device_id_type=MESH,
        )

    d_copy = to_partner(d_own, d_recv, d_s, d_r)
    d_copy.start()

    for copy in proj_copies + x_copies:
        copy.wait()

    @pl.when(has_prev)
    def _():
        for copy in halos:
            copy.wait_recv()

    @pl.when(i == 0)
    def _():
        halo_x[...] = jnp.zeros_like(halo_x)
        halo_p[...] = jnp.zeros_like(halo_p)

    mixed = []
    for k in range(2):
        cols = slice(k * LANES, (k + 1) * LANES)
        mixed.append(
            conv(wide_p, k, halo_p[halo_rows - 8 :, cols], proj_v[k], cp_ref[:, cols])
        )
    write_t = jnp.transpose(mixed[0]).astype(jnp.bfloat16)
    read_vec = mixed[1].astype(jnp.bfloat16)

    def summarize(c):
        cols = pl.ds(pl.multiple_of(c * LANES, LANES), LANES)
        x_c = conv(wide_x, c, halo_x[halo_rows - 8 :, cols], x_v[c], cf_ref[:, cols])
        x_c = x_c.astype(jnp.bfloat16)
        xm[c] = x_c
        weighted = (x_c.astype(jnp.float32) * spread(to_end, c)).astype(jnp.bfloat16)
        return dot(write_t, weighted)

    s_copies = [
        to_partner(s_send.at[j], s_recv.at[j], s_s.at[j], s_r.at[j]) for j in range(half)
    ]
    for j in range(half):
        s_send[j] = summarize((1 - y) * half + j).astype(jnp.bfloat16)
        s_copies[j].start()
    for j in range(half):
        s_own[j] = summarize(y * half + j)

    scores = dot(read_vec, write_t)
    side = LANES
    steps_in = span // side
    causal = iota((side, side), 0) >= iota((side, side), 1)
    low = iota((span, LANES), 1) // width

    def inside(c):
        x_c = xm[c]
        totals = [None] * steps_in
        for q in range(per):
            h = c * per + q
            x_q = jnp.where(low == q, x_c.astype(jnp.float32), 0.0).astype(jnp.bfloat16)
            for r in range(steps_in):
                rows = slice(r * side, (r + 1) * side)
                now = run[rows, h : h + 1]
                tiles = []
                for k in range(r + 1):
                    cols = slice(k * side, (k + 1) * side)
                    gap = now - m_t[h : h + 1, cols]
                    if k == r:
                        gap = jnp.where(causal, gap, -1e30)
                    tiles.append((scores[rows, cols] * jnp.exp2(gap)).astype(jnp.bfloat16))
                mixing = tiles[0] if r == 0 else jnp.concatenate(tiles, axis=1)
                term = dot(mixing, x_q[0 : (r + 1) * side])
                totals[r] = term if totals[r] is None else totals[r] + term
        for r in range(steps_in):
            within[c, r * side : (r + 1) * side] = totals[r]

    @pl.when(i < 2)
    def _():
        p_in[...] = jnp.zeros_like(p_in)

    p_copies = [
        pltpu.make_async_remote_copy(
            src_ref=p_out.at[j],
            dst_ref=p_in.at[j],
            send_sem=p_s.at[j],
            recv_sem=p_r.at[j],
            device_id=(lax.rem(i + 2, n), hd),
            device_id_type=MESH,
        )
        for j in range(half)
    ]
    e_copies = [
        to_partner(e_send.at[j], e_recv.at[j], e_s.at[j], e_r.at[j]) for j in range(half)
    ]

    early = y == 0
    d_copy.wait_recv()
    queue = list(range(chunks))
    for _ in range(2):
        inside(queue.pop(0))
    for j in range(half):
        s_copies[j].wait_recv()

        @pl.when(has_before)
        def _():
            p_copies[j].wait_recv()

        c = y * half + j
        d_mine = d_own[pl.ds(c, 1), :]
        d_other = d_recv[pl.ds(c, 1), :]
        d_first = jnp.where(early, d_mine, d_other)
        d_second = jnp.where(early, d_other, d_mine)
        mine = s_own[j]
        other = s_recv[j].astype(jnp.float32)
        first = jnp.where(early, mine, other)
        second = jnp.where(early, other, mine)
        before = p_in[j].astype(jnp.float32)
        middle = d_first * before + first

        @pl.when(has_after)
        def _():
            p_out[j] = (d_second * middle + second).astype(jnp.bfloat16)
            p_copies[j].start()

        e_own[j] = jnp.where(early, before, middle).astype(jnp.bfloat16)
        e_send[j] = jnp.where(early, middle, before).astype(jnp.bfloat16)
        e_copies[j].start()
        if queue:
            inside(queue.pop(0))
    while queue:
        inside(queue.pop(0))

    for copy in gate_copies:
        copy.wait()
    squares = jnp.zeros((span, LANES), jnp.float32)

    def gate(c, state, squares):
        outside = dot(read_vec, state) * spread(decay_now, c)
        gated = (within[c] + outside) * silu(gate_v[c].astype(jnp.float32))
        within[c] = gated
        return squares + gated * gated

    for j in range(half):
        squares = gate(y * half + j, e_own[j], squares)
    for j in range(half):
        e_copies[j].wait_recv()
        squares = gate((1 - y) * half + j, e_recv[j], squares)

    row = jnp.sum(jnp.transpose(squares), axis=0, keepdims=True)
    sq_send[...] = jnp.broadcast_to(row, sq_send.shape)
    sq_copies = [
        pltpu.make_async_remote_copy(
            src_ref=sq_send,
            dst_ref=sq_recv.at[k - 1],
            send_sem=sq_s.at[k - 1],
            recv_sem=sq_r.at[k - 1],
            device_id=(i, lax.rem(hd + k, m)),
            device_id_type=MESH,
        )
        for k in range(1, m)
    ]
    for copy in sq_copies:
        copy.start()
    for copy in sq_copies:
        copy.wait_recv()
    for k in range(1, m):
        row = row + sq_recv[k - 1, 0:1]
    scale = lax.rsqrt(row / total_channels + 1.0)
    scale = jnp.transpose(jnp.broadcast_to(scale, (LANES, span)))
    for c in range(chunks):
        cols = slice(c * LANES, (c + 1) * LANES)
        out_ref[:, cols] = (within[c] * scale * gain_ref[:, cols]).astype(jnp.bfloat16)

    @pl.when(has_next)
    def _():
        for copy in halos:
            copy.wait_send()

    d_copy.wait_send()
    for copy in s_copies + e_copies + sq_copies:
        copy.wait_send()

    @pl.when(has_after)
    def _():
        for copy in p_copies:
            copy.wait_send()


def shards(n, m, x, gate, proj, raw, bias, rate, cf, cp, gain):
    _, span, channels = x.shape
    heads = rate.shape[0]
    chunks = channels // LANES
    half = chunks // 2
    state = proj.shape[2] // 2
    f32, bf16 = jnp.float32, jnp.bfloat16
    dma = pltpu.SemaphoreType.DMA
    any_spec = pl.BlockSpec(memory_space=pl.ANY)
    vmem = pl.BlockSpec(memory_space=pltpu.VMEM)
    result = pl.pallas_call(
        functools.partial(kernel, n, m, channels * m),
        out_shape=jax.ShapeDtypeStruct((span, channels), bf16),
        in_specs=[any_spec] * 4 + [vmem] * 5,
        out_specs=vmem,
        scratch_shapes=[
            pltpu.VMEM((chunks, span, LANES), bf16),
            pltpu.VMEM((chunks, span, LANES), bf16),
            pltpu.VMEM((2, span, LANES), bf16),
            pltpu.VMEM((span, heads), f32),
            pltpu.VMEM((16, channels), bf16),
            pltpu.VMEM((16, 2 * state), bf16),
            pltpu.VMEM((chunks, span + 8, LANES), f32),
            pltpu.VMEM((2, span + 8, LANES), f32),
            pltpu.VMEM((span, LANES), f32),
            pltpu.VMEM((LANES, span), f32),
            pltpu.VMEM((chunks, span, LANES), bf16),
            pltpu.VMEM((chunks, span, LANES), f32),
            pltpu.VMEM((half, state, LANES), bf16),
            pltpu.VMEM((half, state, LANES), bf16),
            pltpu.VMEM((half, state, LANES), f32),
            pltpu.VMEM((chunks, LANES), f32),
            pltpu.VMEM((chunks, LANES), f32),
            pltpu.VMEM((half, state, LANES), bf16),
            pltpu.VMEM((half, state, LANES), bf16),
            pltpu.VMEM((half, state, LANES), bf16),
            pltpu.VMEM((half, state, LANES), bf16),
            pltpu.VMEM((half, state, LANES), bf16),
            pltpu.VMEM((8, span), f32),
            pltpu.VMEM((m - 1, 8, span), f32),
            dma((chunks,)),
            dma((chunks,)),
            dma((3,)),
            dma((2,)),
            dma((2,)),
            dma,
            dma,
            dma((half,)),
            dma((half,)),
            dma((half,)),
            dma((half,)),
            dma((half,)),
            dma((half,)),
            dma((m - 1,)),
            dma((m - 1,)),
        ],
        compiler_params=pltpu.CompilerParams(collective_id=0, has_side_effects=True),
    )(x[0], gate[0], proj[0], raw[0], bias[None], rate[None], cf, cp, gain[None])
    return result[None]


def solution(mesh):
    sizes = mesh.shape
    return jax.shard_map(
        functools.partial(shards, sizes["seq"], sizes["head"]),
        mesh=mesh,
        in_specs=(
            P(None, "seq", "head"),
            P(None, "seq", "head"),
            P(None, "seq", None),
            P(None, "seq", "head"),
            P("head"),
            P("head"),
            P(None, "head"),
            P(),
            P("head"),
        ),
        out_specs=P(None, "seq", "head"),
        check_vma=False,
    )
```

time: 134 us -> 29.7 us (0.22)
  the two profiles are of different devices: /device:TPU:0 before, /device:TPU:29 now
where the time goes in v1:
time: 29.7 us; the launch traced here: 29.5 us
  Pallas kernels  26.1 us (88%)
  local copies, waits for them, and re-layouts  3.34 us (11%)
    pallas_call x1, Pallas kernels, shards(): pl.pallas_call(functools.partial(kernel, n, m, channels * m), out_shape=j...  26.1 us
    unnamed x2, local copies, waits for them, and re-layouts  3.34 us

profile of v1, /device:TPU:29, one launch (start us, length us, event | category | flops | bytes accessed | tf_op | source)
XLA Modules:
  0.0 29.5 jit_solution(7308867575769761009)
XLA Ops:
  0.0 1.5 %copy.10 = f32[1,256,16]{2,1,0:T(8,128)} copy(f32[1,256,16]{1,2,0:T(8,128)} %param.12) | data formatting | bytes 32768 | tf_op args[3]
  1.5 26.1 %shard_map.91 = bf16[256,1024]{1,0:T(8,128)(2,1)} custom-call(bf16[256,1024]{1,0:T(8,128)(2,1)} %bitcast.9, bf16[256,1024]{1,0:T(8,128)(2,1)} %bitcast.10, bf16[256,256]{1,0:T(8,128)(2,1)} %bitcast.12, f32[256,16]{1,0:T(8,128)} %bitcast.11, f32[1,16]{1,0:T(1,128)} %bitcast.14, f32[1,16]{1,0:T(1,128)} %bitcast.15, f32[4,1024]{1,0:T(4,128)} %cf_ref.1, ...), custom_call_target="tpu_custom_call" | custom-call | tf_op jit(solution)/shard_map/pallas_call | solution.py:409
  27.6 1.9 %copy.12 = bf16[1,256,1024]{2,1,0:T(8,128)(2,1)} copy(bf16[1,256,1024]{2,1,0:T(8,128)(2,1)} %bitcast.8) | data formatting | bytes 1048576

commit v2 on v1

v2 whole, which is shorter than its diff:
```python
import functools
import math

import jax
import jax.numpy as jnp
from jax import lax
from jax.experimental import pallas as pl
from jax.experimental.pallas import tpu as pltpu
from jax.sharding import PartitionSpec as P

HEADS = 64
HEAD_DIM = 64
STRETCH = 256
LANES = 128
LOG2E = math.log2(math.e)
FIX = 16
SPLIT = 2
BEFORE = 4
MESH = pl.DeviceIdType.MESH


def silu(value):
    half = 0.5 * value
    return half + half * jnp.tanh(half)


def pieces(value, count):
    parts = []
    for _ in range(count):
        part = value.astype(jnp.bfloat16)
        parts.append(part)
        value = value - part.astype(jnp.float32)
    return parts


def dot(a, b):
    return jnp.dot(a, b, preferred_element_type=jnp.float32)


def dot_parts(parts, b):
    total = dot(parts[-1], b)
    for part in parts[-2::-1]:
        total = total + dot(part, b)
    return total


def iota(shape, dim):
    return lax.broadcasted_iota(jnp.int32, shape, dim)


def conv(wide, slot, weights, span):
    taps = weights.shape[0]
    first = 8 - taps + 1
    total = wide[slot, first : first + span] * weights[0:1]
    for k in range(1, taps):
        total = total + wide[slot, first + k : first + k + span] * weights[k : k + 1]
    return silu(total)


def kernel(
    n,
    m,
    total_channels,
    x_hbm,
    gate_hbm,
    proj_hbm,
    raw_hbm,
    bias_ref,
    rate_ref,
    cf_ref,
    cp_ref,
    gain_ref,
    out_ref,
    x_v,
    gate_v,
    proj_v,
    raw_v,
    halo_out,
    halo_in,
    wide_x,
    wide_p,
    xm,
    within,
    factor,
    s_part,
    out_v,
    s_send,
    s_recv,
    s_own,
    d_own,
    d_recv,
    p_in,
    p_out,
    e_own,
    e_send,
    e_recv,
    sq_send,
    sq_recv,
    x_sem,
    gate_sem,
    misc_sem,
    out_sem,
    halo_s,
    halo_r,
    d_s,
    d_r,
    s_s,
    s_r,
    p_s,
    p_r,
    e_s,
    e_r,
    sq_s,
    sq_r,
):
    span = proj_v.shape[1]
    chunks = x_v.shape[0]
    half = chunks // 2
    heads = rate_ref.shape[1]
    per = heads // chunks
    width = LANES // per
    i = lax.axis_index("seq")
    hd = lax.axis_index("head")
    y = lax.rem(i, 2)
    partner = i + 1 - 2 * y
    has_prev, has_next = i > 0, i < n - 1
    has_before, has_after = i >= 2, i < n - 2

    barrier = pltpu.get_barrier_semaphore()
    relations = [(has_prev, i - 1), (has_next, i + 1), (has_before, i - 2), (has_after, i + 2)]
    for here, who in relations:

        @pl.when(here)
        def _():
            pl.semaphore_signal(barrier, inc=1, device_id=(who, hd), device_id_type=MESH)

    for k in range(1, m):
        pl.semaphore_signal(
            barrier, inc=1, device_id=(i, lax.rem(hd + k, m)), device_id_type=MESH
        )

    channels = chunks * LANES
    edge = span - halo_in.shape[0]
    edge_copies = [
        pltpu.make_async_copy(
            x_hbm.at[edge:span], halo_out.at[:, 0:channels], misc_sem.at[3]
        ),
        pltpu.make_async_copy(
            proj_hbm.at[edge:span], halo_out.at[:, channels:], misc_sem.at[4]
        ),
    ]
    raw_copy = pltpu.make_async_copy(raw_hbm, raw_v, misc_sem.at[0])
    proj_copies = [
        pltpu.make_async_copy(
            proj_hbm.at[:, k * LANES : (k + 1) * LANES], proj_v.at[k], misc_sem.at[1 + k]
        )
        for k in range(2)
    ]
    for copy in edge_copies + [raw_copy] + proj_copies:
        copy.start()
    x_copies = []
    gate_copies = []
    for c in range(chunks):
        cols = slice(c * LANES, (c + 1) * LANES)
        x_copies.append(pltpu.make_async_copy(x_hbm.at[:, cols], x_v.at[c], x_sem.at[c]))
        gate_copies.append(
            pltpu.make_async_copy(gate_hbm.at[:, cols], gate_v.at[c], gate_sem.at[c])
        )
    for copy in x_copies + gate_copies:
        copy.start()
    for copy in edge_copies:
        copy.wait()

    pl.semaphore_wait(barrier, sum(here.astype(jnp.int32) for here, _ in relations) + m - 1)

    halo_copy = pltpu.make_async_remote_copy(
        src_ref=halo_out,
        dst_ref=halo_in,
        send_sem=halo_s,
        recv_sem=halo_r,
        device_id=(lax.rem(i + 1, n), hd),
        device_id_type=MESH,
    )

    @pl.when(has_next)
    def _():
        halo_copy.start()

    def column(row):
        eye = iota((heads, heads), 0) == iota((heads, heads), 1)
        wide = jnp.broadcast_to(row, (heads, heads))
        return jnp.sum(jnp.where(eye, wide, 0.0), axis=1, keepdims=True)

    raw_copy.wait()
    shifted = raw_v[...] + column(bias_ref[...])
    step = jnp.maximum(shifted, 0.0) + jnp.log1p(jnp.exp(-jnp.abs(shifted)))
    upto = (iota((span, span), 0) <= iota((span, span), 1)).astype(jnp.bfloat16)
    lead = (step * (-LOG2E)) * column(rate_ref[...])
    run_t = dot_parts(pieces(lead, 3), upto)
    source_t = run_t - LOG2E * jnp.log(step)
    last = run_t[:, span - 1 : span]
    to_end = jnp.exp2(last - source_t)
    token = iota((heads, span), 1)
    rows = [
        run_t,
        jnp.where(token < FIX, 0.0, to_end),
        jnp.exp2(run_t),
        jnp.where(token < FIX, to_end, 0.0),
    ]
    rows.append(jnp.zeros((LANES - len(rows) * heads, span), jnp.float32))
    table = jnp.transpose(jnp.concatenate(rows, axis=0))
    run = table
    table_parts = pieces(jnp.where(iota((span, LANES), 1) < heads, 0.0, table), 2)
    fix_parts = [part[0:FIX] for part in table_parts]

    def spread(parts, kind, c):
        source = kind * heads + c * per + iota((LANES, LANES), 1) // width
        return dot_parts(parts, (iota((LANES, LANES), 0) == source).astype(jnp.bfloat16))

    lane_of = iota((heads, LANES), 0) % per == iota((heads, LANES), 1) // width
    ends = jnp.where(lane_of, jnp.exp2(last), 0.0)
    owner = (iota((chunks, heads), 1) // per == iota((chunks, heads), 0)).astype(jnp.bfloat16)
    ends_parts = pieces(ends, 3)
    d_own[...] = dot(owner, ends_parts[2]) + dot(owner, ends_parts[1]) + dot(owner, ends_parts[0])

    def to_partner(src, dst, send_sem, recv_sem):
        return pltpu.make_async_remote_copy(
            src_ref=src,
            dst_ref=dst,
            send_sem=send_sem,
            recv_sem=recv_sem,
            device_id=(partner, hd),
            device_id_type=MESH,
        )

    d_copy = to_partner(d_own, d_recv, d_s, d_r)
    d_copy.start()

    for copy in proj_copies:
        copy.wait()
    mixed = []
    for k in range(2):
        cols = slice(k * LANES, (k + 1) * LANES)
        wide_p[k, 0:8] = jnp.zeros((8, LANES), jnp.float32)
        wide_p[k, 8 : 8 + span] = proj_v[k].astype(jnp.float32)
        mixed.append(conv(wide_p, k, cp_ref[:, cols], span))
    write_t = jnp.transpose(mixed[0])
    write_main = write_t.astype(jnp.bfloat16)

    for c in range(chunks):
        x_copies[c].wait()
        wide_x[c, 0:8] = jnp.zeros((8, LANES), jnp.float32)
        wide_x[c, 8 : 8 + span] = x_v[c].astype(jnp.float32)
        x_c = conv(wide_x, c, cf_ref[:, c * LANES : (c + 1) * LANES], span)
        x_c = x_c.astype(jnp.bfloat16)
        xm[c] = x_c
        weighted = x_c.astype(jnp.float32) * spread(table_parts, 1, c)
        s_part[c] = dot(write_main, weighted.astype(jnp.bfloat16))

    @pl.when(has_prev)
    def _():
        halo_copy.wait_recv()

    @pl.when(i == 0)
    def _():
        halo_in[...] = jnp.zeros_like(halo_in)

    fixed = []
    for k in range(2):
        cols = slice(k * LANES, (k + 1) * LANES)
        lanes = slice(channels + k * LANES, channels + (k + 1) * LANES)
        wide_p[k, 0:8] = halo_in[:, lanes].astype(jnp.float32)
        fixed.append(conv(wide_p, k, cp_ref[:, cols], FIX))
    blank = jnp.zeros((LANES - FIX, LANES), jnp.float32)
    fix_t = jnp.transpose(jnp.concatenate([fixed[0], blank], axis=0))
    fix_write = fix_t[:, 0:FIX].astype(jnp.bfloat16)

    def summarize(c):
        cols = pl.ds(pl.multiple_of(c * LANES, LANES), LANES)
        wide_x[c, 0:8] = halo_in[:, cols].astype(jnp.float32)
        x_c = conv(wide_x, c, cf_ref[:, cols], FIX).astype(jnp.bfloat16)
        xm[c, 0:FIX] = x_c
        weighted = x_c.astype(jnp.float32) * spread(fix_parts, 3, c)
        return s_part[c] + dot(fix_write, weighted.astype(jnp.bfloat16))

    count = half * SPLIT
    tall = s_own.shape[1] // SPLIT
    s_copies = [
        to_partner(s_send.at[j], s_recv.at[j], s_s.at[j], s_r.at[j]) for j in range(count)
    ]
    for j in range(half):
        sent = summarize((1 - y) * half + j).astype(jnp.bfloat16)
        for r in range(SPLIT):
            s_send[j * SPLIT + r] = sent[r * tall : (r + 1) * tall]
            s_copies[j * SPLIT + r].start()
    for j in range(half):
        s_own[j] = summarize(y * half + j)

    head_t = jnp.where(iota((LANES, LANES), 1) < FIX, fix_t, write_t[:, 0:LANES])
    write_t = jnp.concatenate([head_t, write_t[:, LANES:]], axis=1).astype(jnp.bfloat16)
    read_vec = jnp.concatenate([fixed[1], mixed[1][FIX:]], axis=0).astype(jnp.bfloat16)
    scores = dot(read_vec, write_t)
    side = LANES
    steps_in = span // side
    causal = iota((side, side), 0) >= iota((side, side), 1)
    low = iota((span, LANES), 1) // width

    def inside(c):
        x_c = xm[c]
        totals = [None] * steps_in
        for q in range(per):
            h = c * per + q
            x_q = jnp.where(low == q, x_c.astype(jnp.float32), 0.0).astype(jnp.bfloat16)
            for r in range(steps_in):
                rows = slice(r * side, (r + 1) * side)
                now = run[rows, h : h + 1]
                tiles = []
                for k in range(r + 1):
                    cols = slice(k * side, (k + 1) * side)
                    gap = now - source_t[h : h + 1, cols]
                    if k == r:
                        gap = jnp.where(causal, gap, -1e30)
                    tiles.append((scores[rows, cols] * jnp.exp2(gap)).astype(jnp.bfloat16))
                mixing = tiles[0] if r == 0 else jnp.concatenate(tiles, axis=1)
                term = dot(mixing, x_q[0 : (r + 1) * side])
                totals[r] = term if totals[r] is None else totals[r] + term
        gate_copies[c].wait()
        for r in range(steps_in):
            rows = slice(r * side, (r + 1) * side)
            gate = silu(gate_v[c, rows].astype(jnp.float32))
            within[c, rows] = totals[r] * gate
            factor[c, rows] = gate * spread([part[rows] for part in table_parts], 2, c)

    @pl.when(i < 2)
    def _():
        p_in[...] = jnp.zeros_like(p_in)

    p_copies = [
        pltpu.make_async_remote_copy(
            src_ref=p_out.at[j],
            dst_ref=p_in.at[j],
            send_sem=p_s.at[j],
            recv_sem=p_r.at[j],
            device_id=(lax.rem(i + 2, n), hd),
            device_id_type=MESH,
        )
        for j in range(count)
    ]
    e_copies = [
        to_partner(e_send.at[j], e_recv.at[j], e_s.at[j], e_r.at[j]) for j in range(count)
    ]

    early = y == 0
    d_copy.wait_recv()
    queue = list(range(chunks))
    for _ in range(BEFORE):
        inside(queue.pop(0))
    squares = jnp.zeros((span, LANES), jnp.float32)

    def gate_in(c, state, squares):
        gated = within[c] + dot(read_vec, state) * factor[c]
        within[c] = gated
        return squares + gated * gated

    for j in range(half):
        c = y * half + j
        d_mine = d_own[pl.ds(c, 1), :]
        d_other = d_recv[pl.ds(c, 1), :]
        d_first = jnp.where(early, d_mine, d_other)
        d_second = jnp.where(early, d_other, d_mine)
        for r in range(SPLIT):
            k = j * SPLIT + r
            part = slice(r * tall, (r + 1) * tall)
            s_copies[k].wait_recv()
            mine = s_own[j, part]
            other = s_recv[k].astype(jnp.float32)
            first = jnp.where(early, mine, other)
            second = jnp.where(early, other, mine)
            kept = d_second * first + second
            both = d_second * d_first

            @pl.when(has_before)
            def _():
                p_copies[k].wait_recv()

            before = p_in[k].astype(jnp.float32)

            @pl.when(has_after)
            def _():
                p_out[k] = (both * before + kept).astype(jnp.bfloat16)
                p_copies[k].start()

            middle = d_first * before + first
            e_send[k] = jnp.where(early, middle, before).astype(jnp.bfloat16)
            e_copies[k].start()
            e_own[j, part] = jnp.where(early, before, middle).astype(jnp.bfloat16)
        if queue:
            inside(queue.pop(0))
    while queue:
        inside(queue.pop(0))

    for j in range(half):
        squares = gate_in(y * half + j, e_own[j], squares)
    for j in range(half):
        for r in range(SPLIT):
            e_copies[j * SPLIT + r].wait_recv()
        state = jnp.concatenate([e_recv[j * SPLIT + r] for r in range(SPLIT)], axis=0)
        squares = gate_in((1 - y) * half + j, state, squares)

    row = jnp.sum(jnp.transpose(squares), axis=0, keepdims=True)
    sq_send[...] = row
    sq_copies = [
        pltpu.make_async_remote_copy(
            src_ref=sq_send,
            dst_ref=sq_recv.at[k - 1],
            send_sem=sq_s.at[k - 1],
            recv_sem=sq_r.at[k - 1],
            device_id=(i, lax.rem(hd + k, m)),
            device_id_type=MESH,
        )
        for k in range(1, m)
    ]
    for copy in sq_copies:
        copy.start()
    for copy in sq_copies:
        copy.wait_recv()
    for k in range(1, m):
        row = row + sq_recv[k - 1, 0:1]
    scale = lax.rsqrt(row / total_channels + 1.0)
    scale = jnp.transpose(jnp.broadcast_to(scale, (LANES, span)))
    out_copies = []
    for c in range(chunks):
        cols = slice(c * LANES, (c + 1) * LANES)
        out_v[c] = (within[c] * scale * gain_ref[:, cols]).astype(jnp.bfloat16)
        out_copies.append(pltpu.make_async_copy(out_v.at[c], out_ref.at[:, cols], out_sem.at[c]))
        out_copies[c].start()

    @pl.when(has_next)
    def _():
        halo_copy.wait_send()

    d_copy.wait_send()
    for copy in s_copies + e_copies + sq_copies:
        copy.wait_send()

    @pl.when(has_after)
    def _():
        for copy in p_copies:
            copy.wait_send()

    for copy in out_copies:
        copy.wait()


def shards(n, m, x, gate, proj, raw, bias, rate, cf, cp, gain):
    _, span, channels = x.shape
    heads = rate.shape[0]
    chunks = channels // LANES
    state = proj.shape[2] // 2
    half = chunks // 2
    count, tall = half * SPLIT, state // SPLIT
    f32, bf16 = jnp.float32, jnp.bfloat16
    dma = pltpu.SemaphoreType.DMA
    any_spec = pl.BlockSpec(memory_space=pl.ANY)
    vmem = pl.BlockSpec(memory_space=pltpu.VMEM)
    result = pl.pallas_call(
        functools.partial(kernel, n, m, channels * m),
        out_shape=jax.ShapeDtypeStruct((span, channels), bf16),
        in_specs=[any_spec] * 4 + [vmem] * 5,
        out_specs=any_spec,
        scratch_shapes=[
            pltpu.VMEM((chunks, span, LANES), bf16),
            pltpu.VMEM((chunks, span, LANES), bf16),
            pltpu.VMEM((2, span, LANES), bf16),
            pltpu.VMEM((heads, span), f32),
            pltpu.VMEM((8, channels + 2 * state), bf16),
            pltpu.VMEM((8, channels + 2 * state), bf16),
            pltpu.VMEM((chunks, span + 8, LANES), f32),
            pltpu.VMEM((2, span + 8, LANES), f32),
            pltpu.VMEM((chunks, span, LANES), bf16),
            pltpu.VMEM((chunks, span, LANES), f32),
            pltpu.VMEM((chunks, span, LANES), f32),
            pltpu.VMEM((chunks, state, LANES), f32),
            pltpu.VMEM((chunks, span, LANES), bf16),
            pltpu.VMEM((count, tall, LANES), bf16),
            pltpu.VMEM((count, tall, LANES), bf16),
            pltpu.VMEM((half, state, LANES), f32),
            pltpu.VMEM((chunks, LANES), f32),
            pltpu.VMEM((chunks, LANES), f32),
            pltpu.VMEM((count, tall, LANES), bf16),
            pltpu.VMEM((count, tall, LANES), bf16),
            pltpu.VMEM((half, state, LANES), bf16),
            pltpu.VMEM((count, tall, LANES), bf16),
            pltpu.VMEM((count, tall, LANES), bf16),
            pltpu.VMEM((1, span), f32),
            pltpu.VMEM((m - 1, 1, span), f32),
            dma((chunks,)),
            dma((chunks,)),
            dma((5,)),
            dma((chunks,)),
            dma,
            dma,
            dma,
            dma,
            dma((count,)),
            dma((count,)),
            dma((count,)),
            dma((count,)),
            dma((count,)),
            dma((count,)),
            dma((m - 1,)),
            dma((m - 1,)),
        ],
        compiler_params=pltpu.CompilerParams(collective_id=0, has_side_effects=True),
    )(x[0], gate[0], proj[0], jnp.transpose(raw[0]), bias[None], rate[None], cf, cp, gain[None])
    return result[None]


def solution(mesh):
    sizes = mesh.shape
    return jax.shard_map(
        functools.partial(shards, sizes["seq"], sizes["head"]),
        mesh=mesh,
        in_specs=(
            P(None, "seq", "head"),
            P(None, "seq", "head"),
            P(None, "seq", None),
            P(None, "seq", "head"),
            P("head"),
            P("head"),
            P(None, "head"),
            P(),
            P("head"),
        ),
        out_specs=P(None, "seq", "head"),
        check_vma=False,
    )
```

time: 29.7 us -> 28.5 us (0.960)
  the two profiles are of different devices: /device:TPU:29 before, /device:TPU:25 now
where the time goes in v2:
time: 28.5 us; the launch traced here: 28.2 us
  Pallas kernels  26.4 us (93%)
  local copies, waits for them, and re-layouts  1.87 us (7%)
    pallas_call x1, Pallas kernels, shards(): pl.pallas_call(functools.partial(kernel, n, m, channels * m), out_shape=j...  26.4 us
    unnamed x1, local copies, waits for them, and re-layouts  1.87 us

profile of v2, /device:TPU:25, one launch (start us, length us, event | category | flops | bytes accessed | tf_op | source)
XLA Modules:
  0.0 28.2 jit_solution(15048587372545980949)
XLA Ops:
  0.0 26.4 %shard_map.91 = bf16[256,1024]{1,0:T(8,128)(2,1)} custom-call(bf16[256,1024]{1,0:T(8,128)(2,1)} %bitcast.11, bf16[256,1024]{1,0:T(8,128)(2,1)} %bitcast.12, bf16[256,256]{1,0:T(8,128)(2,1)} %bitcast.13, f32[16,256]{1,0:T(8,128)} %bitcast.14, f32[1,16]{1,0:T(1,128)} %bitcast.16, f32[1,16]{1,0:T(1,128)} %bitcast.17, f32[4,1024]{1,0:T(4,128)} %cf_ref.1, ...), custom_call_target="tpu_custom_call" | custom-call | tf_op jit(solution)/shard_map/pallas_call | solution.py:466
  26.4 1.9 %copy.11 = bf16[1,256,1024]{2,1,0:T(8,128)(2,1)} copy(bf16[1,256,1024]{2,1,0:T(8,128)(2,1)} %bitcast.10) | data formatting | bytes 1048576

commit v3 on v2

--- a/solution.py
+++ b/solution.py
@@ -168,24 +168,6 @@
         )
     for copy in x_copies + gate_copies:
         copy.start()
-    for copy in edge_copies:
-        copy.wait()
-
-    pl.semaphore_wait(barrier, sum(here.astype(jnp.int32) for here, _ in relations) + m - 1)
-
-    halo_copy = pltpu.make_async_remote_copy(
-        src_ref=halo_out,
-        dst_ref=halo_in,
-        send_sem=halo_s,
-        recv_sem=halo_r,
-        device_id=(lax.rem(i + 1, n), hd),
-        device_id_type=MESH,
-    )
-
-    @pl.when(has_next)
-    def _():
-        halo_copy.start()
-
     def column(row):
         eye = iota((heads, heads), 0) == iota((heads, heads), 1)
         wide = jnp.broadcast_to(row, (heads, heads))
@@ -210,12 +192,15 @@
     rows.append(jnp.zeros((LANES - len(rows) * heads, span), jnp.float32))
     table = jnp.transpose(jnp.concatenate(rows, axis=0))
     run = table
-    table_parts = pieces(jnp.where(iota((span, LANES), 1) < heads, 0.0, table), 2)
-    fix_parts = [part[0:FIX] for part in table_parts]
-
-    def spread(parts, kind, c):
-        source = kind * heads + c * per + iota((LANES, LANES), 1) // width
-        return dot_parts(parts, (iota((LANES, LANES), 0) == source).astype(jnp.bfloat16))
+
+    def spread(kind, c, rows):
+        first = kind * heads + c * per
+        size = rows.stop - rows.start
+        lane = iota((size, LANES), 1) // width
+        result = jnp.broadcast_to(table[rows, first : first + 1], (size, LANES))
+        for q in range(1, per):
+            result = jnp.where(lane == q, table[rows, first + q : first + q + 1], result)
+        return result
 
     lane_of = iota((heads, LANES), 0) % per == iota((heads, LANES), 1) // width
     ends = jnp.where(lane_of, jnp.exp2(last), 0.0)
@@ -234,6 +219,24 @@
         )
 
     d_copy = to_partner(d_own, d_recv, d_s, d_r)
+    for copy in edge_copies:
+        copy.wait()
+
+    pl.semaphore_wait(barrier, sum(here.astype(jnp.int32) for here, _ in relations) + m - 1)
+
+    halo_copy = pltpu.make_async_remote_copy(
+        src_ref=halo_out,
+        dst_ref=halo_in,
+        send_sem=halo_s,
+        recv_sem=halo_r,
+        device_id=(lax.rem(i + 1, n), hd),
+        device_id_type=MESH,
+    )
+
+    @pl.when(has_next)
+    def _():
+        halo_copy.start()
+
     d_copy.start()
 
     for copy in proj_copies:
@@ -254,7 +257,7 @@
         x_c = conv(wide_x, c, cf_ref[:, c * LANES : (c + 1) * LANES], span)
         x_c = x_c.astype(jnp.bfloat16)
         xm[c] = x_c
-        weighted = x_c.astype(jnp.float32) * spread(table_parts, 1, c)
+        weighted = x_c.astype(jnp.float32) * spread(1, c, slice(0, span))
         s_part[c] = dot(write_main, weighted.astype(jnp.bfloat16))
 
     @pl.when(has_prev)
@@ -275,26 +278,24 @@
     fix_t = jnp.transpose(jnp.concatenate([fixed[0], blank], axis=0))
     fix_write = fix_t[:, 0:FIX].astype(jnp.bfloat16)
 
-    def summarize(c):
-        cols = pl.ds(pl.multiple_of(c * LANES, LANES), LANES)
+    count = half * SPLIT
+    tall = s_recv.shape[1]
+    for c in range(chunks):
+        cols = slice(c * LANES, (c + 1) * LANES)
         wide_x[c, 0:8] = halo_in[:, cols].astype(jnp.float32)
         x_c = conv(wide_x, c, cf_ref[:, cols], FIX).astype(jnp.bfloat16)
         xm[c, 0:FIX] = x_c
-        weighted = x_c.astype(jnp.float32) * spread(fix_parts, 3, c)
-        return s_part[c] + dot(fix_write, weighted.astype(jnp.bfloat16))
-
-    count = half * SPLIT
-    tall = s_own.shape[1] // SPLIT
+        weighted = x_c.astype(jnp.float32) * spread(3, c, slice(0, FIX))
+        whole = s_part[c] + dot(fix_write, weighted.astype(jnp.bfloat16))
+        s_own[c] = whole
+        for r in range(SPLIT):
+            s_send[c * SPLIT + r] = whole[r * tall : (r + 1) * tall].astype(jnp.bfloat16)
     s_copies = [
-        to_partner(s_send.at[j], s_recv.at[j], s_s.at[j], s_r.at[j]) for j in range(count)
-    ]
-    for j in range(half):
-        sent = summarize((1 - y) * half + j).astype(jnp.bfloat16)
-        for r in range(SPLIT):
-            s_send[j * SPLIT + r] = sent[r * tall : (r + 1) * tall]
-            s_copies[j * SPLIT + r].start()
-    for j in range(half):
-        s_own[j] = summarize(y * half + j)
+        to_partner(s_send.at[(1 - y) * count + j], s_recv.at[j], s_s.at[j], s_r.at[j])
+        for j in range(count)
+    ]
+    for copy in s_copies:
+        copy.start()
 
     head_t = jnp.where(iota((LANES, LANES), 1) < FIX, fix_t, write_t[:, 0:LANES])
     write_t = jnp.concatenate([head_t, write_t[:, LANES:]], axis=1).astype(jnp.bfloat16)
@@ -329,7 +330,7 @@
             rows = slice(r * side, (r + 1) * side)
             gate = silu(gate_v[c, rows].astype(jnp.float32))
             within[c, rows] = totals[r] * gate
-            factor[c, rows] = gate * spread([part[rows] for part in table_parts], 2, c)
+            factor[c, rows] = gate * spread(2, c, rows)
 
     @pl.when(i < 2)
     def _():
@@ -359,7 +360,7 @@
 
     def gate_in(c, state, squares):
         gated = within[c] + dot(read_vec, state) * factor[c]
-        within[c] = gated
+        wide_x[c, 8 : 8 + span] = gated
         return squares + gated * gated
 
     for j in range(half):
@@ -372,7 +373,7 @@
             k = j * SPLIT + r
             part = slice(r * tall, (r + 1) * tall)
             s_copies[k].wait_recv()
-            mine = s_own[j, part]
+            mine = s_own[c, part]
             other = s_recv[k].astype(jnp.float32)
             first = jnp.where(early, mine, other)
             second = jnp.where(early, other, mine)
@@ -431,7 +432,7 @@
     out_copies = []
     for c in range(chunks):
         cols = slice(c * LANES, (c + 1) * LANES)
-        out_v[c] = (within[c] * scale * gain_ref[:, cols]).astype(jnp.bfloat16)
+        out_v[c] = (wide_x[c, 8 : 8 + span] * scale * gain_ref[:, cols]).astype(jnp.bfloat16)
         out_copies.append(pltpu.make_async_copy(out_v.at[c], out_ref.at[:, cols], out_sem.at[c]))
         out_copies[c].start()
 
@@ -482,9 +483,9 @@
             pltpu.VMEM((chunks, span, LANES), f32),
             pltpu.VMEM((chunks, state, LANES), f32),
             pltpu.VMEM((chunks, span, LANES), bf16),
+            pltpu.VMEM((2 * count, tall, LANES), bf16),
             pltpu.VMEM((count, tall, LANES), bf16),
-            pltpu.VMEM((count, tall, LANES), bf16),
-            pltpu.VMEM((half, state, LANES), f32),
+            pltpu.VMEM((chunks, state, LANES), f32),
             pltpu.VMEM((chunks, LANES), f32),
             pltpu.VMEM((chunks, LANES), f32),
             pltpu.VMEM((count, tall, LANES), bf16),

time: 28.5 us -> 27.6 us (0.968)
  the two profiles are of different devices: /device:TPU:25 before, /device:TPU:29 now
where the time goes in v3:
time: 27.6 us; the launch traced here: 27.4 us
  Pallas kernels  25.5 us (92%)
  local copies, waits for them, and re-layouts  1.87 us (7%)
    pallas_call x1, Pallas kernels, shards(): pl.pallas_call(functools.partial(kernel, n, m, channels * m), out_shape=j...  25.5 us
    unnamed x1, local copies, waits for them, and re-layouts  1.87 us

profile of v3, /device:TPU:29, one launch (start us, length us, event | category | flops | bytes accessed | tf_op | source)
XLA Modules:
  0.0 27.4 jit_solution(13488955017370361024)
XLA Ops:
  0.0 25.5 %shard_map.91 = bf16[256,1024]{1,0:T(8,128)(2,1)} custom-call(bf16[256,1024]{1,0:T(8,128)(2,1)} %bitcast.11, bf16[256,1024]{1,0:T(8,128)(2,1)} %bitcast.12, bf16[256,256]{1,0:T(8,128)(2,1)} %bitcast.13, f32[16,256]{1,0:T(8,128)} %bitcast.14, f32[1,16]{1,0:T(1,128)} %bitcast.16, f32[1,16]{1,0:T(1,128)} %bitcast.17, f32[4,1024]{1,0:T(4,128)} %cf_ref.1, ...), custom_call_target="tpu_custom_call" | custom-call | tf_op jit(solution)/shard_map/pallas_call | solution.py:467
  25.5 1.9 %copy.11 = bf16[1,256,1024]{2,1,0:T(8,128)(2,1)} copy(bf16[1,256,1024]{2,1,0:T(8,128)(2,1)} %bitcast.10) | data formatting | bytes 1048576
